TPU v7x, 32 devices: a whole 2x2x4 slice. The times are simulated.
32 devices in a mesh: rep: 4 (over x, y), dp: 8 (over z, core).
Axes of the slice: x: 2, y: 2, z: 4, core: 2. Of those that a mesh axis runs over, the one named last changes fastest.
Arguments:
- a: bfloat16 [32, 4, 8192, 1024], P(('rep', 'dp')), parts along dimension 0
- g: bfloat16 [32, 4, 8192, 2560], P(('rep', 'dp')), parts along dimension 0
Outputs:
- output: bfloat16 [16, 1024, 2560], P('rep'), parts along dimension 0
There are 4 independent parts. A program takes and returns all parts, laid end to end along the dimension named above; each array names one.
All inputs are finite; a program needn't handle non-finite values.
Results may differ from a plain program's by a relative error of at most 0.012.
Values are sent between devices in bfloat16 or wider.
A program may use at most 2 GiB of HBM per device.

v0:
```python
import jax
import jax.numpy as jnp


def solution(mesh):
    groups = mesh.shape["rep"]

    def step(a, g):
        a, g = (t.reshape(groups, -1, *t.shape[1:]) for t in (a, g))
        sums = jnp.einsum("rsntd,rsntf->rndf", a, g, preferred_element_type=jnp.float32)
        return sums.astype(jnp.bfloat16).reshape(-1, *sums.shape[2:])

    return step
```

profile of v0, /device:TPU:0, one launch (start us, length us, event | category | flops | bytes accessed | tf_op | source)
XLA Modules:
  0.0 996.0 jit_solution(2831531319432264149)
XLA Ops:
  0.0 187.2 %fusion.3 = f32[1,4,1024,2560]{3,2,1,0:T(8,128)} fusion(bf16[1,4,8192,2560]{3,2,1,0:T(8,128)(2,1)} %param.1, bf16[1,4,8192,1024]{3,2,1,0:T(8,128)(2,1)} %param), kind=kOutput, calls=%fused_computation.3 | convolution fusion | flops 171798691840 | bytes 276824064 | tf_op jit(solution)/rsntd,rsntf->rndf/dot_general | solution.py:10
  187.2 808.8 %all-reduce.2 = bf16[1,4,1024,2560]{3,2,1,0:T(8,128)(2,1)} all-reduce(f32[1,4,1024,2560]{3,2,1,0:T(8,128)} %fusion.3), channel_id=1, replica_groups=[4,8]<=[32], use_global_device_ids=true, to_apply=%add.clone | all-reduce | flops 10485760 | bytes 62914560 | tf_op jit(solution)/rsntd,rsntf->rndf/dot_general | solution.py:10
where the time goes:
time: 999 us; the launch traced here: 996 us
  blocking collectives  809 us (81%)
  matrix products  187 us (19%)
    dot_general x1, blocking collectives, step(): jnp.einsum('rsntd,rsntf->rndf', a, g, preferred_element_type=jnp.float32)  809 us
    dot_general x1, matrix products, step(): jnp.einsum('rsntd,rsntf->rndf', a, g, preferred_element_type=jnp.float32)  187 us

commit v1 on v0

v1 whole, which is shorter than its diff:
```python
import functools

import jax
import jax.numpy as jnp
from jax import lax
from jax.experimental import pallas as pl
from jax.experimental.pallas import tpu as pltpu
from jax.sharding import PartitionSpec as P

MESH = pl.DeviceIdType.MESH
TM, TN = 512, 256
HALF = TM // 2
N_ACC = 6
N_PAIR = 8
N_IN = 16
N_OUT = 8
N_MID = 8
LAG_END, LAG_ADD, LAG_FIN, LAG_FWD = 1, 3, 5, 12


def kernel(shape, a_hbm, g_hbm, out, a_buf, g_buf, acc, pair_out, pair_in, line_out, line_in, mid_in,
           a_sem, g_sem, pair_ssem, pair_rsem, out_ssem, line_rsem, mid_rsem, fin_ssem, fin_rsem, fwd_ssem, fwd_rsem):
    matrices, depth, rows, cols = shape
    per_phase = cols // TN
    phases = matrices * (rows // TM)
    tiles = phases * per_phase
    blocks = rows // TM

    rep, dp = lax.axis_index("rep"), lax.axis_index("dp")
    z, core = dp // 2, dp % 2
    is_end = jnp.logical_or(z == 0, z == 3)
    is_mid = jnp.logical_not(is_end)
    partner = (rep, z * 2 + (1 - core))
    inward = (rep, jnp.where(z < 2, z + 1, z - 1) * 2 + core)
    outward = (rep, jnp.where(z < 2, 0, 3) * 2 + core)
    mine, theirs = core * HALF, (1 - core) * HALF

    def region(ref, t, offset):
        phase = t // per_phase
        row = pl.multiple_of((phase % blocks) * TM + offset, HALF)
        col = pl.multiple_of((t % per_phase) * TN, TN)
        return ref.at[phase // blocks, pl.ds(row, HALF), pl.ds(col, TN)]

    def load_a(p):
        block = pl.multiple_of((p % blocks) * TM, TM)
        return pltpu.make_async_copy(a_hbm.at[p // blocks, :, pl.ds(block, TM)], a_buf.at[p % 2], a_sem.at[p % 2])

    def load_g(t):
        col = pl.multiple_of((t % per_phase) * TN, TN)
        return pltpu.make_async_copy(
            g_hbm.at[t // (per_phase * blocks), :, pl.ds(col, TN)], g_buf.at[t % 2], g_sem.at[t % 2])

    def send(src, dst, ssem, rsem, device):
        return pltpu.make_async_remote_copy(src, dst, ssem, rsem, device_id=device, device_id_type=MESH)

    def pair_copy(t):
        s = t % N_PAIR
        return send(pair_out.at[s], pair_in.at[s], pair_ssem.at[s], pair_rsem.at[s], partner)

    def line_copy(t):
        s, d = t % N_OUT, t % N_IN
        return send(line_out.at[s], line_in.at[d], out_ssem.at[s], line_rsem.at[d], inward)

    def mid_copy(t):
        s, d = t % N_OUT, t % N_MID
        return send(line_out.at[s], mid_in.at[d], out_ssem.at[s], mid_rsem.at[d], inward)

    def fin_copy(t):
        here = region(out, t, mine)
        return send(here, here, fin_ssem, fin_rsem.at[t % N_IN], outward)

    def fwd_copy(t):
        here = region(out, t, mine)
        return send(here, here, fwd_ssem, fwd_rsem, partner)

    load_a(0).start()
    load_g(0).start()
    load_g(1).start()

    barrier = pltpu.get_barrier_semaphore()
    pl.semaphore_signal(barrier, inc=1, device_id=partner, device_id_type=MESH)
    pl.semaphore_signal(barrier, inc=1, device_id=inward, device_id_type=MESH)

    @pl.when(is_mid)
    def _():
        pl.semaphore_signal(barrier, inc=1, device_id=outward, device_id_type=MESH)

    pl.semaphore_wait(barrier, jnp.where(is_mid, 3, 2))

    def compute(t):
        p = t // per_phase

        @pl.when(t % per_phase == 0)
        def _():
            load_a(p).wait()

        load_g(t).wait()
        acc[t % N_ACC] = lax.dot_general(
            a_buf[p % 2], g_buf[t % 2], (((0,), (0,)), ((), ())), preferred_element_type=jnp.float32)

        @pl.when(t + 2 < tiles)
        def _():
            load_g(t + 2).start()

        @pl.when(jnp.logical_and(t % per_phase == 0, p + 1 < phases))
        def _():
            load_a(p + 1).start()

        @pl.when(t >= N_PAIR)
        def _():
            pair_copy(t - N_PAIR).wait_send()

        pair_out[t % N_PAIR] = acc[t % N_ACC, pl.ds(pl.multiple_of(theirs, HALF), HALF)].astype(jnp.bfloat16)
        pair_copy(t).start()

    def chip_sum(t):
        pair_copy(t).wait_recv()
        own = acc[t % N_ACC, pl.ds(pl.multiple_of(mine, HALF), HALF)]
        return own + pair_in[t % N_PAIR].astype(jnp.float32)

    def end_send(t):
        @pl.when(t >= N_OUT)
        def _():
            line_copy(t - N_OUT).wait_send()

        line_out[t % N_OUT] = chip_sum(t).astype(jnp.bfloat16)
        line_copy(t).start()

    def mid_add(t):
        @pl.when(t >= N_OUT)
        def _():
            mid_copy(t - N_OUT).wait_send()

        line_copy(t).wait_recv()
        total = chip_sum(t) + line_in[t % N_IN].astype(jnp.float32)
        line_out[t % N_OUT] = total.astype(jnp.bfloat16)
        mid_copy(t).start()

    def mid_finish(t):
        mid_copy(t).wait_recv()
        total = line_out[t % N_OUT].astype(jnp.float32) + mid_in[t % N_MID].astype(jnp.float32)
        region(out, t, mine)[...] = total.astype(jnp.bfloat16)
        fin_copy(t).start()
        fwd_copy(t).start()

    def end_forward(t):
        fin_copy(t).wait_recv()
        fwd_copy(t).start()

    def between(t, lag, what):
        @pl.when(jnp.logical_and(t >= lag, t < tiles + lag))
        def _():
            what(t - lag)

    def step(t, carry):
        @pl.when(t < tiles)
        def _():
            compute(t)

        @pl.when(is_end)
        def _():
            between(t, LAG_FWD, end_forward)
            between(t, LAG_END, end_send)

        @pl.when(is_mid)
        def _():
            between(t, LAG_ADD, mid_add)
            between(t, LAG_FIN, mid_finish)

        return carry

    lax.fori_loop(0, tiles + LAG_FWD, step, 0)

    for t in range(tiles - N_PAIR, tiles):
        pair_copy(t).wait_send()
    for t in range(tiles - N_OUT, tiles):
        line_copy(t).wait_send()
    half = out.at[pl.ds(0, matrices // 2)]
    whole = send(half, half, fwd_ssem, fwd_rsem, partner)
    whole.wait_send()
    whole.wait_recv()

    @pl.when(is_mid)
    def _():
        send(half, half, fin_ssem, fwd_rsem, outward).wait_send()


def solution(mesh):
    def step(a, g):
        _, matrices, depth, rows = a.shape
        cols = g.shape[-1]
        bf16, f32 = jnp.bfloat16, jnp.float32
        return pl.pallas_call(
            functools.partial(kernel, (matrices, depth, rows, cols)),
            out_shape=pltpu.VMEM((matrices, rows, cols), bf16),
            in_specs=[pl.BlockSpec(memory_space=pltpu.HBM)] * 2,
            out_specs=pl.BlockSpec(memory_space=pltpu.VMEM),
            scratch_shapes=[
                pltpu.VMEM((2, depth, TM), bf16),
                pltpu.VMEM((2, depth, TN), bf16),
                pltpu.VMEM((N_ACC, TM, TN), f32),
                pltpu.VMEM((N_PAIR, HALF, TN), bf16),
                pltpu.VMEM((N_PAIR, HALF, TN), bf16),
                pltpu.VMEM((N_OUT, HALF, TN), bf16),
                pltpu.VMEM((N_IN, HALF, TN), bf16),
                pltpu.VMEM((N_MID, HALF, TN), bf16),
                pltpu.SemaphoreType.DMA((2,)),
                pltpu.SemaphoreType.DMA((2,)),
                pltpu.SemaphoreType.DMA((N_PAIR,)),
                pltpu.SemaphoreType.DMA((N_PAIR,)),
                pltpu.SemaphoreType.DMA((N_OUT,)),
                pltpu.SemaphoreType.DMA((N_IN,)),
                pltpu.SemaphoreType.DMA((N_MID,)),
                pltpu.SemaphoreType.DMA,
                pltpu.SemaphoreType.DMA((N_IN,)),
                pltpu.SemaphoreType.DMA,
                pltpu.SemaphoreType.DMA,
            ],
            compiler_params=pltpu.CompilerParams(
                collective_id=0, has_side_effects=True, vmem_limit_bytes=42 * 2**20),
        )(a[0], g[0])

    return jax.shard_map(
        step, mesh=mesh, in_specs=(P(("rep", "dp")), P(("rep", "dp"))), out_specs=P("rep"), check_vma=False)
```

time: 999 us -> 259 us (0.26)
  blocking collectives: 809 us -> 0 us
  Pallas kernels: 0 us -> 251 us
  matrix products: 187 us -> 0 us
    dot_general x1 -> x0, blocking collectives: 809 us -> none  [step(): jnp.einsum('rsntd,rsntf->rndf', a, g, preferred_element_type=jnp.float32)]
    pallas_call x0 -> x1, Pallas kernels: none -> 251 us  [step(): pl.pallas_call(functools.partial(kernel, (matrices, depth, rows, cols)),...]
    dot_general x1 -> x0, matrix products: 187 us -> none  [step(): jnp.einsum('rsntd,rsntf->rndf', a, g, preferred_element_type=jnp.float32)]
where the time goes in v1:
time: 259 us
  Pallas kernels  251 us (97%)
  local copies, waits for them, and re-layouts  7.54 us (3%)
    pallas_call x1, Pallas kernels, step(): pl.pallas_call(functools.partial(kernel, (matrices, depth, rows, cols)),...  251 us
    unnamed x1, local copies, waits for them, and re-layouts  7.54 us

profile of v1, /device:TPU:0, one launch (start us, length us, event | category | flops | bytes accessed | tf_op | source)
XLA Modules:
  0.0 258.6 jit_solution(10061304662217436684)
XLA Ops:
  0.0 251.0 %shard_map.28 = bf16[4,1024,2560]{2,1,0:T(8,128)(2,1)S(1)} custom-call(bf16[4,8192,1024]{2,1,0:T(8,128)(2,1)} %bitcast.a_hbm, bf16[4,8192,2560]{2,1,0:T(8,128)(2,1)} %bitcast.1.g_hbm), custom_call_target="tpu_custom_call" | custom-call | tf_op jit(solution)/shard_map/pallas_call | solution.py:193
  251.0 7.5 %copy.4 = bf16[4,1024,2560]{2,1,0:T(8,128)(2,1)} copy(bf16[4,1024,2560]{2,1,0:T(8,128)(2,1)S(1)} %shard_map.28) | data formatting | bytes 41943040

commit v2 on v1

v2 whole, which is shorter than its diff:
```python
import functools

import jax
import jax.numpy as jnp
from jax import lax
from jax.experimental import pallas as pl
from jax.experimental.pallas import tpu as pltpu
from jax.sharding import PartitionSpec as P

MESH = pl.DeviceIdType.MESH
TM = 512
STRIP = 128
N_OWN = 8
N_PAIR = 6
N_IN = 10
N_OUT = 4
N_MID = 6
LAG_END, LAG_ADD, LAG_FIN, LAG_FWD = 0, 2, 4, 9
PIECES = 8
FIRST = 4


def kernel(shape, a_hbm, g_hbm, out, a_buf, g_buf, acc, own, pair_out, pair_in, line_out, line_in, mid_in,
           a_sem, g_sem, first_sem, pair_ssem, pair_rsem, out_ssem, line_rsem, mid_rsem, fin_ssem, fin_rsem, fwd_ssem,
           fwd_rsem):
    matrices, depth, rows, cols = shape
    per_phase = cols // (2 * STRIP)
    blocks = rows // TM
    phases = matrices * blocks
    tiles = phases * per_phase

    rep, dp = lax.axis_index("rep"), lax.axis_index("dp")
    z, core = dp // 2, dp % 2
    is_end = jnp.logical_or(z == 0, z == 3)
    is_mid = jnp.logical_not(is_end)
    partner = (rep, z * 2 + (1 - core))
    inward = (rep, jnp.where(z < 2, z + 1, z - 1) * 2 + core)
    outward = (rep, jnp.where(z < 2, 0, 3) * 2 + core)

    def region(t):
        phase = t // per_phase
        row = pl.multiple_of((phase % blocks) * TM, TM)
        col = pl.multiple_of((t % per_phase) * (2 * STRIP) + core * STRIP, STRIP)
        return out.at[phase // blocks, pl.ds(row, TM), pl.ds(col, STRIP)]

    def held(t):
        last = jnp.logical_and(core == 1, t % per_phase == per_phase - 1)
        return jnp.where(last, N_OWN + (t // per_phase) % 2, t % N_OWN)

    def load_a(p, start=0, size=depth):
        block = pl.multiple_of((p % blocks) * TM, TM)
        return pltpu.make_async_copy(
            a_hbm.at[p // blocks, pl.ds(start, size), pl.ds(block, TM)], a_buf.at[p % 2, pl.ds(start, size)],
            a_sem.at[p % 2])

    def load_g(t, strip, start=0, size=depth, sem=None):
        j = t % per_phase
        col = (jnp.where(jnp.logical_and(core == 1, j == 0), per_phase, j) * 2 - core if strip == 0 else j * 2 + 1 - core)
        return pltpu.make_async_copy(
            g_hbm.at[t // (per_phase * blocks), pl.ds(start, size), pl.ds(pl.multiple_of(col * STRIP, STRIP), STRIP)],
            g_buf.at[t % 2, pl.ds(start, size), pl.ds(strip * STRIP, STRIP)], g_sem.at[t % 2] if sem is None else sem)

    def wait_g(t):
        pltpu.make_async_copy(g_buf.at[t % 2], g_buf.at[t % 2], g_sem.at[t % 2]).wait()

    def load_first(k):
        size = depth // FIRST
        part = pl.ds(k * size, size)
        return (pltpu.make_async_copy(a_hbm.at[0, part, pl.ds(0, TM)], a_buf.at[0, part], first_sem.at[0, k]),
                load_g(0, 0, k * size, size, first_sem.at[1, k]), load_g(0, 1, k * size, size, first_sem.at[2, k]))

    def send(src, dst, ssem, rsem, device):
        return pltpu.make_async_remote_copy(src, dst, ssem, rsem, device_id=device, device_id_type=MESH)

    def pair_copy(t):
        s = t % N_PAIR
        return send(pair_out.at[s], pair_in.at[s], pair_ssem.at[s], pair_rsem.at[s], partner)

    def line_copy(t):
        s, d = t % N_OUT, t % N_IN
        return send(line_out.at[s], line_in.at[d], out_ssem.at[s], line_rsem.at[d], inward)

    def mid_copy(t):
        s, d = t % N_OUT, t % N_MID
        return send(line_out.at[s], mid_in.at[d], out_ssem.at[s], mid_rsem.at[d], inward)

    def fin_copy(t):
        return send(region(t), region(t), fin_ssem, fin_rsem.at[t % N_IN], outward)

    def fwd_copy(t):
        return send(region(t), region(t), fwd_ssem, fwd_rsem, partner)

    barrier = pltpu.get_barrier_semaphore()
    pl.semaphore_signal(barrier, inc=1, device_id=partner, device_id_type=MESH)
    pl.semaphore_signal(barrier, inc=1, device_id=inward, device_id_type=MESH)

    @pl.when(is_mid)
    def _():
        pl.semaphore_signal(barrier, inc=1, device_id=outward, device_id_type=MESH)

    def dot(a, g):
        return lax.dot_general(a, g, (((0,), (0,)), ((), ())), preferred_element_type=jnp.float32)

    def compute_first():
        acc[...] = jnp.zeros_like(acc)

        @pl.loop(0, FIRST)
        def _(k):
            for copy in load_first(k):
                copy.wait()
            part = pl.ds(pl.multiple_of(k * (depth // FIRST), depth // FIRST), depth // FIRST)
            acc[...] += dot(a_buf[0, part], g_buf[0, part])

        pl.semaphore_wait(barrier, jnp.where(is_mid, 3, 2))

    def compute_next(t):
        @pl.when(t % per_phase == 0)
        def _():
            load_a(t // per_phase).wait()

        wait_g(t)
        acc[...] = dot(a_buf[(t // per_phase) % 2], g_buf[t % 2])

    def compute(t):
        p, j = t // per_phase, t % per_phase

        @pl.when(t == 0)
        def _():
            compute_first()

        @pl.when(t > 0)
        def _():
            compute_next(t)

        @pl.when(t + 2 < tiles)
        def _():
            load_g(t + 2, 0).start()
            load_g(t + 2, 1).start()

        @pl.when(jnp.logical_and(jnp.logical_and(j > 0, j <= PIECES), p + 1 < phases))
        def _():
            size = depth // PIECES
            load_a(p + 1, pl.multiple_of((j - 1) * size, size), size).start()

        @pl.when(t >= N_PAIR)
        def _():
            pair_copy(t - N_PAIR).wait_send()

        pair_out[t % N_PAIR] = acc[:, STRIP:].astype(jnp.bfloat16)
        pair_copy(t).start()
        mine = jnp.where(core == 0, t, jnp.where(j == 0, t + per_phase - 1, t - 1))
        own[held(mine)] = acc[:, :STRIP]

    def chip_sum(t):
        pair_copy(t).wait_recv()
        return own[held(t)] + pair_in[t % N_PAIR].astype(jnp.float32)

    def end_send(t):
        @pl.when(t >= N_OUT)
        def _():
            line_copy(t - N_OUT).wait_send()

        line_out[t % N_OUT] = chip_sum(t).astype(jnp.bfloat16)
        line_copy(t).start()

    def mid_add(t):
        @pl.when(t >= N_OUT)
        def _():
            mid_copy(t - N_OUT).wait_send()

        line_copy(t).wait_recv()
        total = chip_sum(t) + line_in[t % N_IN].astype(jnp.float32)
        line_out[t % N_OUT] = total.astype(jnp.bfloat16)
        mid_copy(t).start()

    def mid_finish(t):
        mid_copy(t).wait_recv()
        total = line_out[t % N_OUT].astype(jnp.float32) + mid_in[t % N_MID].astype(jnp.float32)
        region(t)[...] = total.astype(jnp.bfloat16)
        fin_copy(t).start()
        fwd_copy(t).start()

    def end_forward(t):
        fin_copy(t).wait_recv()
        fwd_copy(t).start()

    def between(t, lag, what):
        tile = t - lag

        @pl.when(jnp.logical_and(tile >= 0, tile < tiles))
        def _():
            what(tile)

    def step(t, carry):
        @pl.when(t < tiles)
        def _():
            compute(t)

        @pl.when(is_end)
        def _():
            between(t, LAG_END + core, end_send)
            between(t, LAG_FWD, end_forward)

        @pl.when(is_mid)
        def _():
            between(t, LAG_ADD, mid_add)
            between(t, LAG_FIN, mid_finish)

        return carry

    for k in range(FIRST):
        for copy in load_first(k):
            copy.start()
    load_g(1, 0).start()
    load_g(1, 1).start()
    lax.fori_loop(0, tiles + LAG_FWD, step, 0)

    for t in range(tiles - N_PAIR, tiles):
        pair_copy(t).wait_send()
    for t in range(tiles - N_OUT, tiles):
        line_copy(t).wait_send()
    half = out.at[pl.ds(0, matrices // 2)]
    whole = send(half, half, fwd_ssem, fwd_rsem, partner)
    whole.wait_send()
    whole.wait_recv()

    @pl.when(is_mid)
    def _():
        send(half, half, fin_ssem, fwd_rsem, outward).wait_send()


def write_out(held, out, sem):
    matrices = held.shape[0]
    copies = [pltpu.make_async_copy(held.at[n], out.at[n], sem.at[n]) for n in range(matrices)]
    for copy in copies:
        copy.start()
    for copy in copies:
        copy.wait()


def solution(mesh):
    def step(a, g):
        _, matrices, depth, rows = a.shape
        cols = g.shape[-1]
        bf16, f32 = jnp.bfloat16, jnp.float32
        held = pl.pallas_call(
            functools.partial(kernel, (matrices, depth, rows, cols)),
            out_shape=pltpu.VMEM((matrices, rows, cols), bf16),
            in_specs=[pl.BlockSpec(memory_space=pltpu.HBM)] * 2,
            out_specs=pl.BlockSpec(memory_space=pltpu.VMEM),
            scratch_shapes=[
                pltpu.VMEM((2, depth, TM), bf16),
                pltpu.VMEM((2, depth, 2 * STRIP), bf16),
                pltpu.VMEM((TM, 2 * STRIP), f32),
                pltpu.VMEM((N_OWN + 2, TM, STRIP), f32),
                pltpu.VMEM((N_PAIR, TM, STRIP), bf16),
                pltpu.VMEM((N_PAIR, TM, STRIP), bf16),
                pltpu.VMEM((N_OUT, TM, STRIP), bf16),
                pltpu.VMEM((N_IN, TM, STRIP), bf16),
                pltpu.VMEM((N_MID, TM, STRIP), bf16),
                pltpu.SemaphoreType.DMA((2,)),
                pltpu.SemaphoreType.DMA((2,)),
                pltpu.SemaphoreType.DMA((3, FIRST)),
                pltpu.SemaphoreType.DMA((N_PAIR,)),
                pltpu.SemaphoreType.DMA((N_PAIR,)),
                pltpu.SemaphoreType.DMA((N_OUT,)),
                pltpu.SemaphoreType.DMA((N_IN,)),
                pltpu.SemaphoreType.DMA((N_MID,)),
                pltpu.SemaphoreType.DMA,
                pltpu.SemaphoreType.DMA((N_IN,)),
                pltpu.SemaphoreType.DMA,
                pltpu.SemaphoreType.DMA,
            ],
            compiler_params=pltpu.CompilerParams(
                collective_id=0, has_side_effects=True, vmem_limit_bytes=42 * 2**20),
        )(a[0], g[0])
        return pl.pallas_call(
            write_out,
            out_shape=pltpu.HBM((matrices, rows, cols), bf16),
            in_specs=[pl.BlockSpec(memory_space=pl.ANY)],
            out_specs=pl.BlockSpec(memory_space=pltpu.HBM),
            scratch_shapes=[pltpu.SemaphoreType.DMA((matrices,))],
            compiler_params=pltpu.CompilerParams(vmem_limit_bytes=2**20),
        )(held)

    return jax.shard_map(
        step, mesh=mesh, in_specs=(P(("rep", "dp")), P(("rep", "dp"))), out_specs=P("rep"), check_vma=False)
```

time: 259 us -> 256 us (0.988)
  local copies, waits for them, and re-layouts: 7.54 us -> 0 us
  Pallas kernels: 251 us -> 256 us
    unnamed x1 -> x0, local copies, waits for them, and re-layouts: 7.54 us -> none
    pallas_call x0 -> x1, Pallas kernels: none -> 7.27 us  [step(): pl.pallas_call(write_out, out_shape=pltpu.HBM((matrices, rows, cols), bf1...]
    pallas_call x1, Pallas kernels: 251 us -> 248 us  [step(): pl.pallas_call(functools.partial(kernel, (matrices, depth, rows, cols)),...]
where the time goes in v2:
time: 256 us
  Pallas kernels  256 us (100%)
    pallas_call x1, Pallas kernels, step(): pl.pallas_call(functools.partial(kernel, (matrices, depth, rows, cols)),...  248 us
    pallas_call x1, Pallas kernels, step(): pl.pallas_call(write_out, out_shape=pltpu.HBM((matrices, rows, cols), bf1...  7.27 us

profile of v2, /device:TPU:0, one launch (start us, length us, event | category | flops | bytes accessed | tf_op | source)
XLA Modules:
  0.0 255.5 jit_solution(11621658790546318801)
XLA Ops:
  0.0 248.2 %shard_map.28.held = bf16[4,1024,2560]{2,1,0:T(8,128)(2,1)S(1)} custom-call(bf16[4,8192,1024]{2,1,0:T(8,128)(2,1)} %bitcast.a_hbm, bf16[4,8192,2560]{2,1,0:T(8,128)(2,1)} %bitcast.1.g_hbm), custom_call_target="tpu_custom_call" | custom-call | tf_op jit(solution)/shard_map/pallas_call | solution.py:246
  248.2 7.3 %shard_map.29 = bf16[4,1024,2560]{2,1,0:T(8,128)(2,1)} custom-call(bf16[4,1024,2560]{2,1,0:T(8,128)(2,1)S(1)} %shard_map.28.held), custom_call_target="tpu_custom_call" | custom-call | tf_op jit(solution)/shard_map/pallas_call | solution.py:277

commit v3 on v2

--- a/solution.py
+++ b/solution.py
@@ -18,10 +18,12 @@
 LAG_END, LAG_ADD, LAG_FIN, LAG_FWD = 0, 2, 4, 9
 PIECES = 8
 FIRST = 4
-
-
-def kernel(shape, a_hbm, g_hbm, out, a_buf, g_buf, acc, own, pair_out, pair_in, line_out, line_in, mid_in,
-           a_sem, g_sem, first_sem, pair_ssem, pair_rsem, out_ssem, line_rsem, mid_rsem, fin_ssem, fin_rsem, fwd_ssem,
+SECOND = 2
+LAST = 4
+
+
+def kernel(shape, a_hbm, g_hbm, out, a_buf, g_buf, g_late, acc, own, pair_out, pair_in, line_out, line_in, mid_in,
+           a_sem, g_sem, first_sem, second_sem, late_sem, last_rsem, pair_ssem, pair_rsem, out_ssem, in_rsem, mid_rsem, fin_ssem, fwd_ssem,
            fwd_rsem):
     matrices, depth, rows, cols = shape
     per_phase = cols // (2 * STRIP)
@@ -67,7 +69,21 @@
         size = depth // FIRST
         part = pl.ds(k * size, size)
         return (pltpu.make_async_copy(a_hbm.at[0, part, pl.ds(0, TM)], a_buf.at[0, part], first_sem.at[0, k]),
-                load_g(0, 0, k * size, size, first_sem.at[1, k]), load_g(0, 1, k * size, size, first_sem.at[2, k]))
+                load_g(0, 1, k * size, size, first_sem.at[1, k]))
+
+    late = jnp.logical_and(is_end, core == 1)
+
+    def load_first_own(k):
+        size = depth // FIRST
+        return load_g(0, 0, k * size, size, first_sem.at[2, k])
+
+    def load_late():
+        col = (2 * per_phase - 1) * STRIP
+        return pltpu.make_async_copy(g_hbm.at[0, :, pl.ds(col, STRIP)], g_late, late_sem)
+
+    def load_second(k):
+        size = depth // SECOND
+        return load_g(1, 0, k * size, size, second_sem.at[0, k]), load_g(1, 1, k * size, size, second_sem.at[1, k])
 
     def send(src, dst, ssem, rsem, device):
         return pltpu.make_async_remote_copy(src, dst, ssem, rsem, device_id=device, device_id_type=MESH)
@@ -78,17 +94,34 @@
 
     def line_copy(t):
         s, d = t % N_OUT, t % N_IN
-        return send(line_out.at[s], line_in.at[d], out_ssem.at[s], line_rsem.at[d], inward)
+        return send(line_out.at[s], line_in.at[d], out_ssem.at[s], in_rsem.at[d], inward)
 
     def mid_copy(t):
         s, d = t % N_OUT, t % N_MID
         return send(line_out.at[s], mid_in.at[d], out_ssem.at[s], mid_rsem.at[d], inward)
 
     def fin_copy(t):
-        return send(region(t), region(t), fin_ssem, fin_rsem.at[t % N_IN], outward)
+        return send(region(t), region(t), fin_ssem, in_rsem.at[t % N_IN], outward)
 
     def fwd_copy(t):
         return send(region(t), region(t), fwd_ssem, fwd_rsem, partner)
+
+    piece = TM // LAST
+
+    def last_pieces(src, dst, ssem, rsem, device):
+        rows_of = [pl.ds(q * piece, piece) for q in range(LAST)]
+        return [send(src.at[r], dst.at[r], ssem, last_rsem.at[q] if rsem is None else rsem, device)
+                for q, r in enumerate(rows_of)]
+
+    def last_mid():
+        t = tiles - 1
+        return last_pieces(line_out.at[t % N_OUT], mid_in.at[t % N_MID], out_ssem.at[t % N_OUT], None, inward)
+
+    def last_fin():
+        return last_pieces(region(tiles - 1), region(tiles - 1), fin_ssem, None, outward)
+
+    def last_fwd():
+        return last_pieces(region(tiles - 1), region(tiles - 1), fwd_ssem, fwd_rsem, partner)
 
     barrier = pltpu.get_barrier_semaphore()
     pl.semaphore_signal(barrier, inc=1, device_id=partner, device_id_type=MESH)
@@ -101,17 +134,20 @@
     def dot(a, g):
         return lax.dot_general(a, g, (((0,), (0,)), ((), ())), preferred_element_type=jnp.float32)
 
-    def compute_first():
+    def compute_in(pieces, load, slot, own_load=None):
         acc[...] = jnp.zeros_like(acc)
 
-        @pl.loop(0, FIRST)
+        @pl.loop(0, pieces)
         def _(k):
-            for copy in load_first(k):
+            for copy in load(k):
                 copy.wait()
-            part = pl.ds(pl.multiple_of(k * (depth // FIRST), depth // FIRST), depth // FIRST)
-            acc[...] += dot(a_buf[0, part], g_buf[0, part])
-
-        pl.semaphore_wait(barrier, jnp.where(is_mid, 3, 2))
+            if own_load is not None:
+                @pl.when(jnp.logical_not(late))
+                def _():
+                    own_load(k).wait()
+
+            part = pl.ds(pl.multiple_of(k * (depth // pieces), depth // pieces), depth // pieces)
+            acc[...] += dot(a_buf[0, part], g_buf[slot, part])
 
     def compute_next(t):
         @pl.when(t % per_phase == 0)
@@ -126,9 +162,14 @@
 
         @pl.when(t == 0)
         def _():
-            compute_first()
-
-        @pl.when(t > 0)
+            compute_in(FIRST, load_first, 0, load_first_own)
+            pl.semaphore_wait(barrier, jnp.where(is_mid, 3, 2))
+
+        @pl.when(t == 1)
+        def _():
+            compute_in(SECOND, load_second, 1)
+
+        @pl.when(t > 1)
         def _():
             compute_next(t)
 
@@ -171,18 +212,47 @@
         line_copy(t).wait_recv()
         total = chip_sum(t) + line_in[t % N_IN].astype(jnp.float32)
         line_out[t % N_OUT] = total.astype(jnp.bfloat16)
-        mid_copy(t).start()
+
+        @pl.when(t < tiles - 1)
+        def _():
+            mid_copy(t).start()
+
+        @pl.when(t == tiles - 1)
+        def _():
+            for copy in last_mid():
+                copy.start()
 
     def mid_finish(t):
-        mid_copy(t).wait_recv()
-        total = line_out[t % N_OUT].astype(jnp.float32) + mid_in[t % N_MID].astype(jnp.float32)
-        region(t)[...] = total.astype(jnp.bfloat16)
-        fin_copy(t).start()
-        fwd_copy(t).start()
+        @pl.when(t < tiles - 1)
+        def _():
+            mid_copy(t).wait_recv()
+            total = line_out[t % N_OUT].astype(jnp.float32) + mid_in[t % N_MID].astype(jnp.float32)
+            region(t)[...] = total.astype(jnp.bfloat16)
+            fin_copy(t).start()
+            fwd_copy(t).start()
+
+        @pl.when(t == tiles - 1)
+        def _():
+            for q, (mid, fin, fwd) in enumerate(zip(last_mid(), last_fin(), last_fwd())):
+                mid.wait_recv()
+                here = pl.ds(q * piece, piece)
+                total = (line_out[(tiles - 1) % N_OUT, here].astype(jnp.float32)
+                         + mid_in[(tiles - 1) % N_MID, here].astype(jnp.float32))
+                region(tiles - 1).at[here][...] = total.astype(jnp.bfloat16)
+                fin.start()
+                fwd.start()
 
     def end_forward(t):
-        fin_copy(t).wait_recv()
-        fwd_copy(t).start()
+        @pl.when(t < tiles - 1)
+        def _():
+            fin_copy(t).wait_recv()
+            fwd_copy(t).start()
+
+        @pl.when(t == tiles - 1)
+        def _():
+            for fin, fwd in zip(last_fin(), last_fwd()):
+                fin.wait_recv()
+                fwd.start()
 
     def between(t, lag, what):
         tile = t - lag
@@ -200,6 +270,15 @@
         def _():
             between(t, LAG_END + core, end_send)
             between(t, LAG_FWD, end_forward)
+
+        @pl.when(jnp.logical_and(late, t == 1))
+        def _():
+            load_late().start()
+
+        @pl.when(jnp.logical_and(late, t == per_phase - 1))
+        def _():
+            load_late().wait()
+            own[held(per_phase - 1)] = dot(a_buf[0], g_late[...])
 
         @pl.when(is_mid)
         def _():
@@ -211,8 +290,19 @@
     for k in range(FIRST):
         for copy in load_first(k):
             copy.start()
-    load_g(1, 0).start()
-    load_g(1, 1).start()
+
+        @pl.when(jnp.logical_not(late))
+        def _(k=k):
+            load_first_own(k).start()
+
+    for k in range(SECOND):
+        for copy in load_second(k):
+            copy.start()
+
+    @pl.when(late)
+    def _():
+        g_buf[0, :, :STRIP] = jnp.zeros((depth, STRIP), g_buf.dtype)
+
     lax.fori_loop(0, tiles + LAG_FWD, step, 0)
 
     for t in range(tiles - N_PAIR, tiles):
@@ -251,6 +341,7 @@
             scratch_shapes=[
                 pltpu.VMEM((2, depth, TM), bf16),
                 pltpu.VMEM((2, depth, 2 * STRIP), bf16),
+                pltpu.VMEM((depth, STRIP), bf16),
                 pltpu.VMEM((TM, 2 * STRIP), f32),
                 pltpu.VMEM((N_OWN + 2, TM, STRIP), f32),
                 pltpu.VMEM((N_PAIR, TM, STRIP), bf16),
@@ -261,13 +352,15 @@
                 pltpu.SemaphoreType.DMA((2,)),
                 pltpu.SemaphoreType.DMA((2,)),
                 pltpu.SemaphoreType.DMA((3, FIRST)),
+                pltpu.SemaphoreType.DMA((2, SECOND)),
+                pltpu.SemaphoreType.DMA,
+                pltpu.SemaphoreType.DMA((LAST,)),
                 pltpu.SemaphoreType.DMA((N_PAIR,)),
                 pltpu.SemaphoreType.DMA((N_PAIR,)),
                 pltpu.SemaphoreType.DMA((N_OUT,)),
                 pltpu.SemaphoreType.DMA((N_IN,)),
                 pltpu.SemaphoreType.DMA((N_MID,)),
                 pltpu.SemaphoreType.DMA,
-                pltpu.SemaphoreType.DMA((N_IN,)),
                 pltpu.SemaphoreType.DMA,
                 pltpu.SemaphoreType.DMA,
             ],

time: 256 us -> 255 us (level)
  no operation moved by 1% of the time
where the time goes in v3:
time: 255 us
  Pallas kernels  255 us (100%)
    pallas_call x1, Pallas kernels, step(): pl.pallas_call(functools.partial(kernel, (matrices, depth, rows, cols)),...  247 us
    pallas_call x1, Pallas kernels, step(): pl.pallas_call(write_out, out_shape=pltpu.HBM((matrices, rows, cols), bf1...  7.27 us

profile of v3, /device:TPU:0, one launch (start us, length us, event | category | flops | bytes accessed | tf_op | source)
XLA Modules:
  0.0 254.7 jit_solution(11270212380592191188)
XLA Ops:
  0.0 247.5 %shard_map.28.held = bf16[4,1024,2560]{2,1,0:T(8,128)(2,1)S(1)} custom-call(bf16[4,8192,1024]{2,1,0:T(8,128)(2,1)} %bitcast.a_hbm, bf16[4,8192,2560]{2,1,0:T(8,128)(2,1)} %bitcast.1.g_hbm), custom_call_target="tpu_custom_call" | custom-call | tf_op jit(solution)/shard_map/pallas_call | solution.py:336
  247.5 7.3 %shard_map.29 = bf16[4,1024,2560]{2,1,0:T(8,128)(2,1)} custom-call(bf16[4,1024,2560]{2,1,0:T(8,128)(2,1)S(1)} %shard_map.28.held), custom_call_target="tpu_custom_call" | custom-call | tf_op jit(solution)/shard_map/pallas_call | solution.py:370

commit v4 on v3

--- a/solution.py
+++ b/solution.py
@@ -19,7 +19,7 @@
 PIECES = 8
 FIRST = 4
 SECOND = 2
-LAST = 4
+LAST = 2
 
 
 def kernel(shape, a_hbm, g_hbm, out, a_buf, g_buf, g_late, acc, own, pair_out, pair_in, line_out, line_in, mid_in,
@@ -83,7 +83,9 @@
 
     def load_second(k):
         size = depth // SECOND
-        return load_g(1, 0, k * size, size, second_sem.at[0, k]), load_g(1, 1, k * size, size, second_sem.at[1, k])
+        part = pl.ds(k * size, size)
+        cols_of = pl.ds(pl.multiple_of((2 - core) * STRIP, STRIP), 2 * STRIP)
+        return (pltpu.make_async_copy(g_hbm.at[0, part, cols_of], g_buf.at[1, part], second_sem.at[k]),)
 
     def send(src, dst, ssem, rsem, device):
         return pltpu.make_async_remote_copy(src, dst, ssem, rsem, device_id=device, device_id_type=MESH)
@@ -352,7 +354,7 @@
                 pltpu.SemaphoreType.DMA((2,)),
                 pltpu.SemaphoreType.DMA((2,)),
                 pltpu.SemaphoreType.DMA((3, FIRST)),
-                pltpu.SemaphoreType.DMA((2, SECOND)),
+                pltpu.SemaphoreType.DMA((SECOND,)),
                 pltpu.SemaphoreType.DMA,
                 pltpu.SemaphoreType.DMA((LAST,)),
                 pltpu.SemaphoreType.DMA((N_PAIR,)),

time: 255 us -> 255 us (level)
  no operation moved by 1% of the time
where the time goes in v4:
time: 255 us
  Pallas kernels  255 us (100%)
    pallas_call x1, Pallas kernels, step(): pl.pallas_call(functools.partial(kernel, (matrices, depth, rows, cols)),...  247 us
    pallas_call x1, Pallas kernels, step(): pl.pallas_call(write_out, out_shape=pltpu.HBM((matrices, rows, cols), bf1...  7.27 us

profile of v4, /device:TPU:0, one launch (start us, length us, event | category | flops | bytes accessed | tf_op | source)
XLA Modules:
  0.0 254.8 jit_solution(8101056000764019435)
XLA Ops:
  0.0 247.5 %shard_map.28.held = bf16[4,1024,2560]{2,1,0:T(8,128)(2,1)S(1)} custom-call(bf16[4,8192,1024]{2,1,0:T(8,128)(2,1)} %bitcast.a_hbm, bf16[4,8192,2560]{2,1,0:T(8,128)(2,1)} %bitcast.1.g_hbm), custom_call_target="tpu_custom_call" | custom-call | tf_op jit(solution)/shard_map/pallas_call | solution.py:338
  247.5 7.3 %shard_map.29 = bf16[4,1024,2560]{2,1,0:T(8,128)(2,1)} custom-call(bf16[4,1024,2560]{2,1,0:T(8,128)(2,1)S(1)} %shard_map.28.held), custom_call_target="tpu_custom_call" | custom-call | tf_op jit(solution)/shard_map/pallas_call | solution.py:372
